TPU v7x, 256 devices: a whole 4x4x8 slice. The times are simulated.
256 devices in a mesh: blk: 128 (over y, x_lo, z, core), shard: 2 (over x_hi).
Axes of the slice: x: 4 (x_hi: 2, x_lo: 2; x = x_hi * 2 + x_lo), y: 4, z: 8, core: 2. Of those that a mesh axis runs over, the one named last changes fastest.
Arguments:
- cut_acts: bfloat16 [65536, 1024], P('blk'), may hold values from -6 to 6
- upstream: bfloat16 [65536, 1024], P('blk', 'shard'), may hold values from -1 to 1
- weights: bfloat16 [128, 1024, 1024], P('blk', None, 'shard'), may hold values from -0.59765625 to 0.59765625
- moment_one: float32 [128, 1024, 1024], P('blk', None, 'shard'), may hold values from -6 to 6
- moment_two: float32 [128, 1024, 1024], P('blk', None, 'shard'), may hold values from 1 to 8
Outputs:
- new_weights: bfloat16 [128, 1024, 1024], P('blk', None, 'shard')
- new_moment_one: float32 [128, 1024, 1024], P('blk', None, 'shard')
- new_moment_two: float32 [128, 1024, 1024], P('blk', None, 'shard')
- cut_grads: bfloat16 [3, 65536, 1024], P(None, ('blk', 'shard'))
All inputs are finite; a program needn't handle non-finite values.
Results may differ from a plain program's by a relative error of at most 0.0074.
Values may be sent and summed in bfloat16 or wider, within the bound.
A program may use at most 64 MiB of HBM per device.

v0:
```python
import jax
import jax.numpy as jnp
from jax import lax
from jax.sharding import PartitionSpec as P

HOPS = 3


def in_blocks(shard, dim, devices):
    before, after = (shard.shape[:dim], shard.shape[dim + 1 :])
    return jnp.moveaxis(shard.reshape(*before, devices, -1, *after), dim, 0)


def sent_and_summed(shard, axis, dim):
    devices = lax.axis_size(axis)
    pieces = lax.all_to_all(in_blocks(shard, dim, devices), axis, 0, 0, tiled=True)
    return jnp.sum(pieces.astype(jnp.float32), axis=0)


def passed_along(shard, axis, by):
    devices = lax.axis_size(axis)
    return lax.ppermute(shard, axis, [(i, (i + by) % devices) for i in range(devices)])


def gelu_slope(values):
    inner = 0.7978845608 * (values + 0.044715 * values * values * values)
    tanh_part = jnp.tanh(inner)
    return 0.5 * (1.0 + tanh_part) + 0.5 * values * (1.0 - tanh_part * tanh_part) * 0.7978845608 * (
        1.0 + 0.134145 * values * values
    )


def train_local(kernel, first, second, inputs, grad_out):
    preact = jnp.dot(inputs, kernel, preferred_element_type=jnp.float32)
    slopes = (grad_out.astype(jnp.float32) * gelu_slope(preact)).astype(jnp.bfloat16)
    gradient = lax.dot_general(
        inputs, slopes, (((0,), (0,)), ((), ())), preferred_element_type=jnp.float32
    )
    returned = sent_and_summed(
        lax.dot_general(
            slopes, kernel, (((1,), (1,)), ((), ())), preferred_element_type=jnp.float32
        ).astype(jnp.bfloat16),
        "shard",
        0,
    ).astype(jnp.bfloat16)
    first = 0.9 * first + 0.1 * gradient
    second = 0.95 * second + 0.05 * gradient * gradient
    kernel = (kernel.astype(jnp.float32) - 0.01 * first / (jnp.sqrt(second) + 1e-08)).astype(
        jnp.bfloat16
    )
    return (kernel, first, second, returned)


def shards(cut_acts, upstream, weights, moment_one, moment_two):
    kernel = weights[0]
    first = moment_one[0]
    second = moment_two[0]
    returned_all = []
    for hop_index in range(HOPS):
        kernel, first, second, returned = train_local(kernel, first, second, cut_acts, upstream)
        kernel = passed_along(kernel, "blk", 1)
        first, second = (
            passed_along(first.astype(jnp.bfloat16), "blk", 1).astype(first.dtype),
            passed_along(second.astype(jnp.bfloat16), "blk", 1).astype(second.dtype),
        )
        returned_all.append(returned)
    return (kernel[None], first[None], second[None], jnp.stack(returned_all))


def solution(mesh):
    placed = (
        P("blk", None),
        P("blk", "shard"),
        P("blk", None, "shard"),
        P("blk", None, "shard"),
        P("blk", None, "shard"),
    )
    return jax.shard_map(
        shards,
        mesh=mesh,
        in_specs=placed,
        out_specs=(
            P("blk", None, "shard"),
            P("blk", None, "shard"),
            P("blk", None, "shard"),
            P(None, ("blk", "shard"), None),
        ),
        check_vma=False,
    )
```

profile of v0, /device:TPU:0, one launch (start us, length us, event | category | flops | bytes accessed | tf_op | source)
XLA Modules:
  0.0 191.2 jit_solution(8480394753653206683)
XLA Ops:
  0.7 2.4 %copy.9 = bf16[1,1024,512]{1,2,0:T(8,128)(2,1)} copy(bf16[1,1024,512]{2,1,0:T(8,128)(2,1)} %param.7) | data formatting | bytes 2097152 | tf_op args[2]
  3.1 1.8 copy.10
  4.9 1.9 %copy.11 = f32[1,1024,512]{1,2,0:T(8,128)S(1)} copy(f32[1,1024,512]{2,1,0:T(8,128)} %param.9) | data formatting | bytes 4194304 | tf_op args[4]
  6.8 2.8 %fusion.10 = bf16[512,512]{1,0:T(8,128)(2,1)S(1)} fusion(bf16[512,512]{1,0:T(8,128)(2,1)} %param.6, bf16[512,1024]{1,0:T(8,128)(2,1)S(1)} %copy-done, bf16[1,1024,512]{2,1,0:T(8,128)(2,1)} %param.7), kind=kOutput, calls=%fused_computation.34 | convolution fusion | flops 542113792 | bytes 3145728 | tf_op jit(solution)/shard_map/dot_general | solution.py:34
  9.7 2.0 %fusion.34 = (bf16[1024,512]{0,1:T(8,128)(2,1)S(1)}, bf16[1024,512]{0,1:T(8,128)(2,1)S(1)}, bf16[1024,512]{0,1:T(8,128)(2,1)S(1)}) fusion(f32[1,1024,512]{1,2,0:T(8,128)S(1)} %copy.11, f32[1,1024,512]{1,2,0:T(8,128)S(1)} %copy-done.2, bf16[1,1024,512]{1,2,0:T(8,128)(2,1)S(1)} %copy-done.4, bf16[512,512]{1,0:T(8,128)(2,1)S(1)} %fusion.10, ...), kind=kOutput, calls=%fused_computation.58 | convolution fusion | flops 544735232 | bytes 9961472 | tf_op jit(solution)/shard_map/dot_general | solution.py:36
  12.1 19.0 %collective-permute-done = bf16[1024,512]{0,1:T(8,128)(2,1)S(1)} collective-permute-done((bf16[1024,512]{0,1:T(8,128)(2,1)S(1)}, bf16[1024,512]{0,1:T(8,128)(2,1)S(1)}, u32[]{:S(2)}, u32[]{:S(2)}) %collective-permute-start) | collective-permute-done | bytes 1048608 | tf_op jit(solution)/shard_map/ppermute | solution.py:22
  31.2 1.3 fusion.11
  32.5 9.9 %collective-permute-done.2 = bf16[1024,512]{0,1:T(8,128)(2,1)S(1)} collective-permute-done((bf16[1024,512]{0,1:T(8,128)(2,1)S(1)}, bf16[1024,512]{0,1:T(8,128)(2,1)S(1)}, u32[]{:S(2)}, u32[]{:S(2)}) %collective-permute-start.2) | collective-permute-done | bytes 1048608 | tf_op jit(solution)/shard_map/ppermute | solution.py:22
  42.4 11.2 %collective-permute-done.1 = bf16[1024,512]{0,1:T(8,128)(2,1)S(1)} collective-permute-done((bf16[1024,512]{0,1:T(8,128)(2,1)S(1)}, bf16[1024,512]{0,1:T(8,128)(2,1)S(1)}, u32[]{:S(2)}, u32[]{:S(2)}) %collective-permute-start.1) | collective-permute-done | bytes 1048608 | tf_op jit(solution)/shard_map/ppermute | solution.py:22
  53.6 3.7 %fusion.9 = (bf16[1024,512]{0,1:T(8,128)(2,1)}, bf16[1024,512]{0,1:T(8,128)(2,1)}, bf16[1024,512]{0,1:T(8,128)(2,1)}) fusion(bf16[1024,512]{0,1:T(8,128)(2,1)S(1)} %collective-permute-done.2, bf16[1024,512]{0,1:T(8,128)(2,1)S(1)} %collective-permute-done.1, bf16[1024,512]{0,1:T(8,128)(2,1)S(1)} %collective-permute-done, bf16[512,512]{1,0:T(8,128)(2,1)S(1)} %fusion.11, ...), kind=kOutput, calls=%fused_computation.33 | convolution fusion | flops 545783808 | bytes 7864320 | tf_op jit(solution)/shard_map/dot_general | solution.py:36
  57.7 1.7 convolution_convert_fusion.2
  59.4 4.4 %all-to-all-start = ((bf16[2,256,1024]{2,1,0:T(8,128)(2,1)}), bf16[2,256,1024]{2,1,0:T(8,128)(2,1)}, u32[]{:S(2)}, u32[]{:S(2)}) async-start(bf16[2,256,1024]{2,1,0:T(8,128)(2,1)} %bitcast.11), calls=%async_computation | async-start | bytes 2097152 | tf_op jit(solution)/shard_map/all_to_all | solution.py:16
  63.8 2.8 %convolution_convert_fusion.1 = bf16[512,1024]{1,0:T(8,128)(2,1)} fusion(bf16[512,512]{1,0:T(8,128)(2,1)} %copy-done.11, bf16[1024,512]{0,1:T(8,128)(2,1)S(1)} %collective-permute-done), kind=kOutput, calls=%fused_computation.26 | convolution fusion | flops 537395200 | bytes 2621440 | tf_op jit(solution)/shard_map/dot_general | solution.py:40
  66.6 9.5 %collective-permute-done.3 = bf16[1024,512]{0,1:T(8,128)(2,1)S(1)} collective-permute-done((bf16[1024,512]{0,1:T(8,128)(2,1)}, bf16[1024,512]{0,1:T(8,128)(2,1)S(1)}, u32[]{:S(2)}, u32[]{:S(2)}) %collective-permute-start.3) | collective-permute-done | bytes 1048608 | tf_op jit(solution)/shard_map/ppermute | solution.py:22
  76.1 1.0 copy-done.5
  77.1 1.3 fusion.12
  79.9 26.9 %all-to-all-done = bf16[2,256,1024]{2,1,0:T(8,128)(2,1)} async-done(((bf16[2,256,1024]{2,1,0:T(8,128)(2,1)}), bf16[2,256,1024]{2,1,0:T(8,128)(2,1)}, u32[]{:S(2)}, u32[]{:S(2)}) %all-to-all-start) | async-done | bytes 1048608 | tf_op jit(solution)/shard_map/all_to_all | solution.py:16
  106.8 4.4 %all-to-all-start.1 = ((bf16[2,256,1024]{2,1,0:T(8,128)(2,1)}), bf16[2,256,1024]{2,1,0:T(8,128)(2,1)}, u32[]{:S(2)}, u32[]{:S(2)}) async-start(bf16[2,256,1024]{2,1,0:T(8,128)(2,1)} %bitcast.101), calls=%async_computation.1 | async-start | bytes 2097152 | tf_op jit(solution)/shard_map/all_to_all | solution.py:16
  111.3 5.3 %fusion.8 = (bf16[1024,512]{0,1:T(8,128)(2,1)}, bf16[1024,512]{0,1:T(8,128)(2,1)}, bf16[1024,512]{0,1:T(8,128)(2,1)}) fusion(f32[512,1024]{1,0:T(8,128)S(1)} %fusion.35, bf16[1024,512]{0,1:T(8,128)(2,1)} %collective-permute-done.5, bf16[1024,512]{0,1:T(8,128)(2,1)} %collective-permute-done.4, bf16[1024,512]{0,1:T(8,128)(2,1)} %copy-done.5), kind=kLoop, calls=%fused_computation.32 | loop fusion | flops 8912896 | bytes 8388608 | tf_op jit(solution)/shard_map/convert_element_type | solution.py:64
  116.6 1.7 convolution_convert_fusion
  118.3 42.2 %all-to-all-done.1 = bf16[2,256,1024]{2,1,0:T(8,128)(2,1)} async-done(((bf16[2,256,1024]{2,1,0:T(8,128)(2,1)}), bf16[2,256,1024]{2,1,0:T(8,128)(2,1)}, u32[]{:S(2)}, u32[]{:S(2)}) %all-to-all-start.1) | async-done | bytes 1048608 | tf_op jit(solution)/shard_map/all_to_all | solution.py:16
  160.6 3.6 %all-to-all-start.2 = ((bf16[2,256,1024]{2,1,0:T(8,128)(2,1)}), bf16[2,256,1024]{2,1,0:T(8,128)(2,1)S(1)}, u32[]{:S(2)}, u32[]{:S(2)}) async-start(bf16[2,256,1024]{2,1,0:T(8,128)(2,1)} %bitcast.15), calls=%async_computation.2 | async-start | bytes 2097152 | tf_op jit(solution)/shard_map/all_to_all | solution.py:16
  164.2 1.5 reduce_sum.36
  165.6 1.5 reduce_sum.37
  167.1 11.7 %all-to-all-done.2 = bf16[2,256,1024]{2,1,0:T(8,128)(2,1)S(1)} async-done(((bf16[2,256,1024]{2,1,0:T(8,128)(2,1)}), bf16[2,256,1024]{2,1,0:T(8,128)(2,1)S(1)}, u32[]{:S(2)}, u32[]{:S(2)}) %all-to-all-start.2) | async-done | bytes 1048608 | tf_op jit(solution)/shard_map/all_to_all | solution.py:16
  178.8 1.1 reduce_sum.38
  180.0 2.4 %pad_maximum_fusion = bf16[3,256,1024]{2,1,0:T(8,128)(2,1)} fusion(bf16[1,256,1024]{2,1,0:T(8,128)(2,1)} %bitcast.100, bf16[1,256,1024]{2,1,0:T(8,128)(2,1)S(1)} %bitcast.99, bf16[1,256,1024]{2,1,0:T(8,128)(2,1)S(1)} %bitcast.98), kind=kLoop, calls=%fused_computation.15 | loop fusion | flops 1572864 | bytes 3145728 | tf_op jit(solution)/shard_map/stack | solution.py:67
  182.3 1.5 bitcast_convert_fusion
  183.8 1.8 copy.16
  185.6 2.3 %copy.14 = bf16[1,1024,512]{2,1,0:T(8,128)(2,1)} copy(bf16[1,1024,512]{1,2,0:T(8,128)(2,1)} %bitcast.8) | data formatting | bytes 2097152
  187.9 1.5 bitcast_convert_fusion.1
  189.4 1.8 copy.15
  (38 shorter events, 2.4 us)
Async XLA Ops:
  0.6 6.2 %copy-start = (bf16[512,1024]{1,0:T(8,128)(2,1)S(1)}, bf16[512,1024]{1,0:T(8,128)(2,1)}, u32[]{:S(2)}) copy-start(bf16[512,1024]{1,0:T(8,128)(2,1)} %param.5) | copy-start | bytes 3145732
  0.6 2.4 %copy-start.1 = (f32[1,1024,512]{2,1,0:T(8,128)S(1)}, f32[1,1024,512]{2,1,0:T(8,128)}, u32[]{:S(2)}) copy-start(f32[1,1024,512]{2,1,0:T(8,128)} %param.8) | copy-start | bytes 6291460
  6.8 2.8 %copy-start.2 = (f32[1,1024,512]{1,2,0:T(8,128)S(1)}, f32[1,1024,512]{1,2,0:T(8,128)}, u32[]{:S(2)}) copy-start(f32[1,1024,512]{1,2,0:T(8,128)} %copy.10) | copy-start | bytes 6291460
  6.8 2.8 %copy-start.4 = (bf16[1,1024,512]{1,2,0:T(8,128)(2,1)S(1)}, bf16[1,1024,512]{1,2,0:T(8,128)(2,1)}, u32[]{:S(2)}) copy-start(bf16[1,1024,512]{1,2,0:T(8,128)(2,1)} %copy.9) | copy-start | bytes 3145732
  9.7 21.5 %copy-start.9 = (bf16[512,512]{1,0:T(8,128)(2,1)S(1)}, bf16[512,512]{1,0:T(8,128)(2,1)}, u32[]{:S(2)}) copy-start(bf16[512,512]{1,0:T(8,128)(2,1)} %param.6) | copy-start | bytes 1572868
  11.6 19.5 %collective-permute-start = (bf16[1024,512]{0,1:T(8,128)(2,1)S(1)}, bf16[1024,512]{0,1:T(8,128)(2,1)S(1)}, u32[]{:S(2)}, u32[]{:S(2)}) collective-permute-start(bf16[1024,512]{0,1:T(8,128)(2,1)S(1)} %get-tuple-element.9), channel_id=1, source_target_pairs={{0,2},{2,4},{4,6},{6,8},{8,10},{10,12},{12,14},{14,16},{16,18},{18... | collective-permute-start | bytes 3145736 | tf_op jit(solution)/shard_map/ppermute | solution.py:22
  11.7 30.7 %collective-permute-start.2 = (bf16[1024,512]{0,1:T(8,128)(2,1)S(1)}, bf16[1024,512]{0,1:T(8,128)(2,1)S(1)}, u32[]{:S(2)}, u32[]{:S(2)}) collective-permute-start(bf16[1024,512]{0,1:T(8,128)(2,1)S(1)} %get-tuple-element.8), channel_id=1, source_target_pairs={{0,2},{2,4},{4,6},{6,8},{8,10},{10,12},{12,14},{14,16},{16,18},{18... | collective-permute-start | bytes 3145736 | tf_op jit(solution)/shard_map/ppermute | solution.py:22
  12.0 41.6 %collective-permute-start.1 = (bf16[1024,512]{0,1:T(8,128)(2,1)S(1)}, bf16[1024,512]{0,1:T(8,128)(2,1)S(1)}, u32[]{:S(2)}, u32[]{:S(2)}) collective-permute-start(bf16[1024,512]{0,1:T(8,128)(2,1)S(1)} %get-tuple-element.10), channel_id=1, source_target_pairs={{0,2},{2,4},{4,6},{6,8},{8,10},{10,12},{12,14},{14,16},{16,18},{18... | collective-permute-start | bytes 3145736 | tf_op jit(solution)/shard_map/ppermute | solution.py:22
  32.5 24.9 %copy-start.11 = (bf16[512,512]{1,0:T(8,128)(2,1)}, bf16[512,512]{1,0:T(8,128)(2,1)S(1)}, u32[]{:S(2)}) copy-start(bf16[512,512]{1,0:T(8,128)(2,1)S(1)} %fusion.11) | copy-start | bytes 1572868
  32.5 25.2 %copy-start.3 = (bf16[1,1024,512]{2,1,0:T(8,128)(2,1)S(1)}, bf16[1,1024,512]{2,1,0:T(8,128)(2,1)}, u32[]{:S(2)}) copy-start(bf16[1,1024,512]{2,1,0:T(8,128)(2,1)} %param.7) | copy-start | bytes 3145732
  57.4 18.8 %collective-permute-start.3 = (bf16[1024,512]{0,1:T(8,128)(2,1)}, bf16[1024,512]{0,1:T(8,128)(2,1)S(1)}, u32[]{:S(2)}, u32[]{:S(2)}) collective-permute-start(bf16[1024,512]{0,1:T(8,128)(2,1)} %get-tuple-element.15), channel_id=1, source_target_pairs={{0,2},{2,4},{4,6},{6,8},{8,10},{10,12},{12,14},{14,16},{16,18},{18... | collective-permute-start | bytes 3145736 | tf_op jit(solution)/shard_map/ppermute | solution.py:22
  57.4 53.9 %collective-permute-start.5 = (bf16[1024,512]{0,1:T(8,128)(2,1)}, bf16[1024,512]{0,1:T(8,128)(2,1)}, u32[]{:S(2)}, u32[]{:S(2)}) collective-permute-start(bf16[1024,512]{0,1:T(8,128)(2,1)} %get-tuple-element.14), channel_id=1, source_target_pairs={{0,2},{2,4},{4,6},{6,8},{8,10},{10,12},{12,14},{14,16},{16,18},{18... | collective-permute-start | bytes 3145736 | tf_op jit(solution)/shard_map/ppermute | solution.py:22
  57.4 53.9 %collective-permute-start.4 = (bf16[1024,512]{0,1:T(8,128)(2,1)}, bf16[1024,512]{0,1:T(8,128)(2,1)}, u32[]{:S(2)}, u32[]{:S(2)}) collective-permute-start(bf16[1024,512]{0,1:T(8,128)(2,1)} %get-tuple-element.16), channel_id=1, source_target_pairs={{0,2},{2,4},{4,6},{6,8},{8,10},{10,12},{12,14},{14,16},{16,18},{18... | collective-permute-start | bytes 3145736 | tf_op jit(solution)/shard_map/ppermute | solution.py:22
  59.4 47.4 %all-to-all-start = ((bf16[2,256,1024]{2,1,0:T(8,128)(2,1)}), bf16[2,256,1024]{2,1,0:T(8,128)(2,1)}, u32[]{:S(2)}, u32[]{:S(2)}) async-start(bf16[2,256,1024]{2,1,0:T(8,128)(2,1)} %bitcast.11), calls=%async_computation | async-start | bytes 2097152 | tf_op jit(solution)/shard_map/all_to_all | solution.py:16
  63.8 13.3 %copy-start.10 = (bf16[512,512]{1,0:T(8,128)(2,1)S(1)}, bf16[512,512]{1,0:T(8,128)(2,1)}, u32[]{:S(2)}) copy-start(bf16[512,512]{1,0:T(8,128)(2,1)} %param.6) | copy-start | bytes 1572868
  76.1 1.0 copy-start.5
  78.4 0.8 copy-start.7
  106.8 53.8 %all-to-all-start.1 = ((bf16[2,256,1024]{2,1,0:T(8,128)(2,1)}), bf16[2,256,1024]{2,1,0:T(8,128)(2,1)}, u32[]{:S(2)}, u32[]{:S(2)}) async-start(bf16[2,256,1024]{2,1,0:T(8,128)(2,1)} %bitcast.101), calls=%async_computation.1 | async-start | bytes 2097152 | tf_op jit(solution)/shard_map/all_to_all | solution.py:16
  111.2 5.4 %copy-start.6 = (bf16[1024,512]{0,1:T(8,128)(2,1)S(1)}, bf16[1024,512]{0,1:T(8,128)(2,1)}, u32[]{:S(2)}) copy-start(bf16[1024,512]{0,1:T(8,128)(2,1)} %copy-done.5) | copy-start | bytes 3145732
  111.2 5.4 %copy-start.8 = (bf16[512,512]{1,0:T(8,128)(2,1)S(1)}, bf16[512,512]{1,0:T(8,128)(2,1)}, u32[]{:S(2)}) copy-start(bf16[512,512]{1,0:T(8,128)(2,1)} %copy-done.7) | copy-start | bytes 1572868
  116.5 65.8 %collective-permute-start.8 = (bf16[1024,512]{0,1:T(8,128)(2,1)}, bf16[1024,512]{0,1:T(8,128)(2,1)}, u32[]{:S(2)}, u32[]{:S(2)}) collective-permute-start(bf16[1024,512]{0,1:T(8,128)(2,1)} %get-tuple-element.11), channel_id=1, source_target_pairs={{0,2},{2,4},{4,6},{6,8},{8,10},{10,12},{12,14},{14,16},{16,18},{18... | collective-permute-start | bytes 3145736 | tf_op jit(solution)/shard_map/ppermute | solution.py:22
  116.5 69.1 %collective-permute-start.6 = (bf16[1024,512]{0,1:T(8,128)(2,1)}, bf16[1024,512]{0,1:T(8,128)(2,1)}, u32[]{:S(2)}, u32[]{:S(2)}) collective-permute-start(bf16[1024,512]{0,1:T(8,128)(2,1)} %get-tuple-element.12), channel_id=1, source_target_pairs={{0,2},{2,4},{4,6},{6,8},{8,10},{10,12},{12,14},{14,16},{16,18},{18... | collective-permute-start | bytes 3145736 | tf_op jit(solution)/shard_map/ppermute | solution.py:22
  116.5 71.4 %collective-permute-start.7 = (bf16[1024,512]{0,1:T(8,128)(2,1)}, bf16[1024,512]{0,1:T(8,128)(2,1)}, u32[]{:S(2)}, u32[]{:S(2)}) collective-permute-start(bf16[1024,512]{0,1:T(8,128)(2,1)} %get-tuple-element.13), channel_id=1, source_target_pairs={{0,2},{2,4},{4,6},{6,8},{8,10},{10,12},{12,14},{14,16},{16,18},{18... | collective-permute-start | bytes 3145736 | tf_op jit(solution)/shard_map/ppermute | solution.py:22
  160.6 18.3 %all-to-all-start.2 = ((bf16[2,256,1024]{2,1,0:T(8,128)(2,1)}), bf16[2,256,1024]{2,1,0:T(8,128)(2,1)S(1)}, u32[]{:S(2)}, u32[]{:S(2)}) async-start(bf16[2,256,1024]{2,1,0:T(8,128)(2,1)} %bitcast.15), calls=%async_computation.2 | async-start | bytes 2097152 | tf_op jit(solution)/shard_map/all_to_all | solution.py:16
where the time goes:
time: 195 us; the launch traced here: 191 us
  waiting for transfers between devices  131 us (67%)
  matrix products  18 us (9%)
  other arithmetic  14.6 us (7%)
  local copies, waits for them, and re-layouts  13.9 us (7%)
  starting transfers between devices  13.3 us (7%)
    all_to_all x3, waiting for transfers between devices, sent_and_summed(): lax.all_to_all(in_blocks(shard, dim, devices), axis, 0, 0, tiled=True)  80.9 us
    ppermute x9, waiting for transfers between devices, passed_along(): lax.ppermute(shard, axis, [(i, (i + by) % devices) for i in range(devices)])  49.7 us
    unnamed x30, local copies, waits for them, and re-layouts  13.9 us
    all_to_all x3, starting transfers between devices, sent_and_summed(): lax.all_to_all(in_blocks(shard, dim, devices), axis, 0, 0, tiled=True)  12.4 us
    dot_general x3, matrix products, train_local(): lax.dot_general(inputs, slopes, (((0,), (0,)), ((), ())), preferred_eleme...  6.41 us
    dot_general x3, matrix products, train_local(): lax.dot_general(slopes, kernel, (((1,), (1,)), ((), ())), preferred_eleme...  6.19 us
    dot_general x3, matrix products, train_local(): preact = jnp.dot(inputs, kernel, preferred_element_type=jnp.float32)  5.39 us
    convert_element_type x1, other arithmetic, shards(): second.astype(jnp.bfloat16)  5.26 us
  transfers between devices with their start and end apart: 12, of which 7 were waited for; matrix products, arithmetic and copies ran while one was open for 14% of the time, Pallas kernels for 0%

commit v1 on v0

v1 whole, which is shorter than its diff:
```python
import functools

import jax
import jax.numpy as jnp
from jax import lax
from jax.experimental import pallas as pl
from jax.experimental.pallas import tpu as pltpu
from jax.sharding import PartitionSpec as P

HOPS = 3
D = 1024
N = 512
ROWS = 512
HALF = ROWS // 2
C = 128
Q = N // C
RB = 4
RR = D // RB
RELAYED = 2
Z = 8
MESH = pl.DeviceIdType.MESH
F32 = jnp.float32
BF16 = jnp.bfloat16


def gelu_slope(values):
    square = values * values
    inner = 0.7978845608 * (values + 0.044715 * square * values)
    tanh_part = jnp.tanh(inner)
    return 0.5 * (1.0 + tanh_part) + 0.5 * values * (1.0 - tanh_part * tanh_part) * 0.7978845608 * (
        1.0 + 0.134145 * square
    )


def kernel(
    acts_hbm,
    up_hbm,
    w_hbm,
    m_hbm,
    v_hbm,
    w_out,
    m_out,
    v_out,
    cut_out,
    x_ref,
    xt_ref,
    g_ref,
    w0_ref,
    m0_ref,
    v0_ref,
    arrived,
    leaving,
    relay,
    s_ref,
    own,
    theirs,
    given,
    x_sem,
    g_sem,
    w_sem,
    m_sem,
    v_sem,
    send_sem,
    recv_sem,
    relay_send_sem,
    relay_recv_sem,
    cut_send_sem,
    cut_recv_sem,
):
    n_blk = lax.axis_size("blk")
    me = lax.axis_index("blk")
    side = lax.axis_index("shard")
    after = lax.rem(me + 1, n_blk)
    before = lax.rem(me + n_blk - 1, n_blk)
    on_chip = lax.rem(me, 2)
    depth = lax.rem(me // 2, Z)
    turns = jnp.logical_and(on_chip == 1, depth == Z - 1)
    relays = jnp.logical_and(on_chip == 0, depth == Z - 1)
    lands = jnp.logical_and(on_chip == 0, depth == 0)
    via = lax.rem(me + 2 * Z - 1, n_blk)
    source = lax.rem(me + n_blk - 2 * Z + 1, n_blk)
    landing = lax.rem(me + n_blk - 2 * (Z - 1), n_blk)
    relayer = lax.rem(me + 2 * (Z - 1), n_blk)

    barrier = pltpu.get_barrier_semaphore()

    def greet(index):
        pl.semaphore_signal(barrier, inc=1, device_id={"blk": index}, device_id_type=MESH)

    greet(after)
    greet(before)
    pl.semaphore_signal(barrier, inc=1, device_id={"shard": 1 - side}, device_id_type=MESH)

    @pl.when(turns)
    def _():
        greet(via)

    @pl.when(relays)
    def _():
        greet(source)
        greet(landing)

    @pl.when(lands)
    def _():
        greet(relayer)

    def columns(q):
        return pl.ds(pl.multiple_of(q * C, C), C)

    def load_x():
        return pltpu.make_async_copy(acts_hbm, x_ref, x_sem)

    def load_w(q):
        return pltpu.make_async_copy(w_hbm.at[0, :, columns(q)], w0_ref.at[q], w_sem.at[q])

    def load_g(q):
        return pltpu.make_async_copy(up_hbm.at[:, columns(q)], g_ref.at[q], g_sem.at[q])

    def load_m(q):
        return pltpu.make_async_copy(m_hbm.at[0, :, columns(q)], m0_ref.at[q], m_sem.at[q])

    def load_v(q):
        return pltpu.make_async_copy(v_hbm.at[0, :, columns(q)], v0_ref.at[q], v_sem.at[q])

    load_x().start()
    for q in range(Q):
        load_w(q).start()
        load_g(q).start()
        load_m(q).start()
        load_v(q).start()

    def rows(r):
        return slice(r * RR, (r + 1) * RR)

    def onward(h, q, r):
        return pltpu.make_async_remote_copy(
            src_ref=leaving.at[h, q, :, rows(r)],
            dst_ref=arrived.at[h, q, :, rows(r)],
            send_sem=send_sem.at[h, q, r],
            recv_sem=recv_sem.at[h, q, r],
            device_id={"blk": after},
            device_id_type=MESH,
        )

    def to_relay(h, q, r):
        return pltpu.make_async_remote_copy(
            src_ref=leaving.at[h, q, :, rows(r)],
            dst_ref=relay.at[h, q, r - RB + RELAYED],
            send_sem=send_sem.at[h, q, r],
            recv_sem=relay_recv_sem.at[h, q, r - RB + RELAYED],
            device_id={"blk": via},
            device_id_type=MESH,
        )

    def from_relay(h, q, r):
        return pltpu.make_async_remote_copy(
            src_ref=relay.at[h, q, r - RB + RELAYED],
            dst_ref=arrived.at[h, q, :, rows(r)],
            send_sem=relay_send_sem.at[h, q, r - RB + RELAYED],
            recv_sem=recv_sem.at[h, q, r],
            device_id={"blk": landing},
            device_id_type=MESH,
        )

    def send(h, q, r):
        if r < RB - RELAYED:
            onward(h, q, r).start()
        else:

            @pl.when(turns)
            def _():
                to_relay(h, q, r).start()

            @pl.when(jnp.logical_not(turns))
            def _():
                onward(h, q, r).start()

    def pass_on(h, q):
        @pl.when(relays)
        def _():
            for r in range(RB - RELAYED, RB):
                to_relay(h, q, r).wait_recv()
                from_relay(h, q, r).start()

    def slopes(q, weight):
        preact = jnp.dot(x_ref[...], weight, preferred_element_type=F32)
        s_ref[q] = (g_ref[q].astype(F32) * gelu_slope(preact)).astype(BF16)

    def update(h, q, r, weight, first, second):
        grad = jnp.dot(xt_ref[rows(r), :], s_ref[q], preferred_element_type=F32)
        first = 0.9 * first + 0.1 * grad
        second = 0.95 * second + 0.05 * grad * grad
        leaving[h, q, 0, rows(r)] = (weight.astype(F32) - 0.01 * first / (jnp.sqrt(second) + 1e-08)).astype(BF16)
        leaving[h, q, 1, rows(r)] = first.astype(BF16)
        leaving[h, q, 2, rows(r)] = second.astype(BF16)
        send(h, q, r)

    def cut(h):
        return pltpu.make_async_remote_copy(
            src_ref=given.at[h],
            dst_ref=theirs.at[h],
            send_sem=cut_send_sem.at[h],
            recv_sem=cut_recv_sem.at[h],
            device_id={"shard": 1 - side},
            device_id_type=MESH,
        )

    def cut_part(weights, start, block):
        s_part = jnp.concatenate([s_ref[q, pl.ds(start, HALF), :] for q in range(Q)], axis=1)
        w_part = jnp.concatenate([weights(q)[rows(block), :] for q in range(Q)], axis=1)
        return lax.dot_general(s_part, w_part, (((1,), (1,)), ((), ())), preferred_element_type=F32)

    def cut_grads(h, weights):
        mine = pl.multiple_of(side * HALF, HALF)
        others = pl.multiple_of((1 - side) * HALF, HALF)
        for block in range(RB):
            given[h, :, rows(block)] = cut_part(weights, others, block).astype(BF16)
        cut(h).start()
        for block in range(RB):
            own[h, :, rows(block)] = cut_part(weights, mine, block)

    def cut_done(h):
        cut(h).wait_recv()
        cut_out[h] = (own[h] + theirs[h].astype(F32)).astype(BF16)

    load_x().wait()

    def hop_start(q):
        load_w(q).wait()
        load_g(q).wait()
        slopes(q, w0_ref[q])

    def hop_rest(q):
        load_m(q).wait()
        load_v(q).wait()
        for r in range(RB):
            update(0, q, r, w0_ref[q, rows(r)], m0_ref[q, rows(r)], v0_ref[q, rows(r)])

    hop_start(0)
    for r in range(RB):
        xt_ref[rows(r), :] = x_ref[:, rows(r)].T
    pl.semaphore_wait(
        barrier,
        3 + turns.astype(jnp.int32) + 2 * relays.astype(jnp.int32) + lands.astype(jnp.int32),
    )
    hop_rest(0)

    @pl.loop(1, Q)
    def _(q):
        hop_start(q)
        hop_rest(q)

    cut_grads(0, lambda q: w0_ref.at[q])

    for h in range(1, HOPS):

        @pl.loop(0, Q)
        def _(q):
            pass_on(h - 1, q)
            for r in range(RB):
                onward(h - 1, q, r).wait_recv()
            slopes(q, arrived[h - 1, q, 0])
            for r in range(RB):
                update(
                    h,
                    q,
                    r,
                    arrived[h - 1, q, 0, rows(r)],
                    arrived[h - 1, q, 1, rows(r)].astype(F32),
                    arrived[h - 1, q, 2, rows(r)].astype(F32),
                )

        cut_grads(h, lambda q: arrived.at[h - 1, q, 0])
        cut_done(h - 1)

    def settle(q):
        pass_on(HOPS - 1, q)
        for r in range(RB):
            onward(HOPS - 1, q, r).wait_recv()
            w_out[rows(r), columns(q)] = arrived[HOPS - 1, q, 0, rows(r)]
            m_out[rows(r), columns(q)] = arrived[HOPS - 1, q, 1, rows(r)].astype(F32)
            v_out[rows(r), columns(q)] = arrived[HOPS - 1, q, 2, rows(r)].astype(F32)

    @pl.loop(0, 2)
    def _(q):
        settle(q)

    cut_done(HOPS - 1)

    @pl.loop(2, Q)
    def _(q):
        settle(q)

    for h in range(HOPS):
        cut(h).wait_send()

        @pl.loop(0, Q)
        def _(q):
            for r in range(RB):
                onward(h, q, r).wait_send()

            @pl.when(relays)
            def _():
                for r in range(RB - RELAYED, RB):
                    from_relay(h, q, r).wait_send()


def shards(cut_acts, upstream, weights, moment_one, moment_two):
    anywhere = pl.BlockSpec(memory_space=pl.ANY)
    held = pl.BlockSpec(memory_space=pltpu.VMEM)
    kernel_out, first, second, cuts = pl.pallas_call(
        kernel,
        out_shape=(
            pltpu.VMEM((D, N), BF16),
            pltpu.VMEM((D, N), F32),
            pltpu.VMEM((D, N), F32),
            pltpu.VMEM((HOPS, HALF, D), BF16),
        ),
        in_specs=[anywhere] * 5,
        out_specs=(held,) * 4,
        scratch_shapes=[
            pltpu.VMEM((ROWS, D), BF16),
            pltpu.VMEM((D, ROWS), BF16),
            pltpu.VMEM((Q, ROWS, C), BF16),
            pltpu.VMEM((Q, D, C), BF16),
            pltpu.VMEM((Q, D, C), F32),
            pltpu.VMEM((Q, D, C), F32),
            pltpu.VMEM((HOPS, Q, 3, D, C), BF16),
            pltpu.VMEM((HOPS, Q, 3, D, C), BF16),
            pltpu.VMEM((HOPS, Q, RELAYED, 3, RR, C), BF16),
            pltpu.VMEM((Q, ROWS, C), BF16),
            pltpu.VMEM((HOPS, HALF, D), F32),
            pltpu.VMEM((HOPS, HALF, D), BF16),
            pltpu.VMEM((HOPS, HALF, D), BF16),
            pltpu.SemaphoreType.DMA,
            pltpu.SemaphoreType.DMA((Q,)),
            pltpu.SemaphoreType.DMA((Q,)),
            pltpu.SemaphoreType.DMA((Q,)),
            pltpu.SemaphoreType.DMA((Q,)),
            pltpu.SemaphoreType.DMA((HOPS, Q, RB)),
            pltpu.SemaphoreType.DMA((HOPS, Q, RB)),
            pltpu.SemaphoreType.DMA((HOPS, Q, RELAYED)),
            pltpu.SemaphoreType.DMA((HOPS, Q, RELAYED)),
            pltpu.SemaphoreType.DMA((HOPS,)),
            pltpu.SemaphoreType.DMA((HOPS,)),
        ],
        compiler_params=pltpu.CompilerParams(
            collective_id=0, has_side_effects=True, vmem_limit_bytes=48 * 2**20
        ),
        name="relay_train",
    )(cut_acts, upstream, weights, moment_one, moment_two)
    return kernel_out[None], first[None], second[None], cuts


def solution(mesh):
    placed = (
        P("blk", None),
        P("blk", "shard"),
        P("blk", None, "shard"),
        P("blk", None, "shard"),
        P("blk", None, "shard"),
    )
    return jax.shard_map(
        shards,
        mesh=mesh,
        in_specs=placed,
        out_specs=(
            P("blk", None, "shard"),
            P("blk", None, "shard"),
            P("blk", None, "shard"),
            P(None, ("blk", "shard"), None),
        ),
        check_vma=False,
    )
```

time: 195 us -> 119 us (0.61)
  waiting for transfers between devices: 131 us -> 0 us
  Pallas kernels: 0 us -> 112 us
  matrix products: 18 us -> 0 us
  other arithmetic: 14.6 us -> 0 us
  starting transfers between devices: 13.3 us -> 0 us
  local copies, waits for them, and re-layouts: 13.9 us -> 4.75 us
    pallas_call x0 -> x1, Pallas kernels: none -> 112 us  [shards(): pl.pallas_call(kernel, out_shape=(pltpu.VMEM((D, N), BF16), pltpu.VMEM((D...]
    all_to_all x3 -> x0, waiting for transfers between devices: 80.9 us -> none  [sent_and_summed(): lax.all_to_all(in_blocks(shard, dim, devices), axis, 0, 0, tiled=True)]
    ppermute x9 -> x0, waiting for transfers between devices: 49.7 us -> none  [passed_along(): lax.ppermute(shard, axis, [(i, (i + by) % devices) for i in range(devices)])]
    dot_general x9 -> x0, matrix products: 18 us -> none  [the longest x3 6.41 us: train_local(): lax.dot_general(inputs, slopes, (((0,), (0,)), ((), ())), preferred_eleme...]
    all_to_all x3 -> x0, starting transfers between devices: 12.4 us -> none  [sent_and_summed(): lax.all_to_all(in_blocks(shard, dim, devices), axis, 0, 0, tiled=True)]
    unnamed x30 -> x4, local copies, waits for them, and re-layouts: 13.9 us -> 4.75 us
    convert_element_type x1 -> x0, other arithmetic: 5.26 us -> none  [shards(): second.astype(jnp.bfloat16)]
    reduce_sum x3 -> x0, other arithmetic: 4.09 us -> none  [sent_and_summed(): return jnp.sum(pieces.astype(jnp.float32), axis=0)]
  transfers between devices with their start and end apart: 12 -> 0, of which waited for: 7 -> 0; matrix products, arithmetic and copies ran while one was open for 14% -> 0% of each run, Pallas kernels for 0% -> 0%
where the time goes in v1:
time: 119 us; the launch traced here: 117 us
  Pallas kernels  112 us (94%)
  local copies, waits for them, and re-layouts  4.75 us (4%)
    pallas_call x1, Pallas kernels, shards(): pl.pallas_call(kernel, out_shape=(pltpu.VMEM((D, N), BF16), pltpu.VMEM((D...  112 us
    unnamed x4, local copies, waits for them, and re-layouts  4.75 us

profile of v1, /device:TPU:0, one launch (start us, length us, event | category | flops | bytes accessed | tf_op | source)
XLA Modules:
  0.0 117.1 jit_solution(14369568188224865258)
XLA Ops:
  0.6 111.7 %relay_train.1 = (bf16[1024,512]{1,0:T(8,128)(2,1)S(1)}, f32[1024,512]{1,0:T(8,128)S(1)}, f32[1024,512]{1,0:T(8,128)S(1)}, bf16[3,256,1024]{2,1,0:T(8,128)(2,1)S(1)}) custom-call(bf16[512,1024]{1,0:T(8,128)(2,1)} %acts_hbm.1, bf16[512,512]{1,0:T(8,128)(2,1)} %up_hbm.1, bf16[1,1024,512]{2,1,0:T(8,128)(2,1)} %w_hbm.1, f32[1,1024,512]{2,1,0:T(8,128)} %m_hbm.1, ...), custom_call_target="tpu_custom_call" | custom-call | tf_op jit(solution)/shard_map/relay_train/pallas_call | solution.py:311
  112.3 1.0 copy.13
  113.3 1.3 %copy.14 = f32[1,1024,512]{2,1,0:T(8,128)} copy(f32[1,1024,512]{2,1,0:T(8,128)S(1)} %bitcast.4) | data formatting | bytes 4194304
  114.6 1.1 copy.16
  115.8 1.3 %copy.15 = f32[1,1024,512]{2,1,0:T(8,128)} copy(f32[1,1024,512]{2,1,0:T(8,128)S(1)} %bitcast.3) | data formatting | bytes 4194304

commit v2 on v1

--- a/solution.py
+++ b/solution.py
@@ -16,8 +16,10 @@
 Q = N // C
 RB = 4
 RR = D // RB
-RELAYED = 2
+RELAYED = 3
+TURNED = (2, 2)
 Z = 8
+BACKWARD = (2, 2, 1)
 MESH = pl.DeviceIdType.MESH
 F32 = jnp.float32
 BF16 = jnp.bfloat16
@@ -51,6 +53,7 @@
     arrived,
     leaving,
     relay,
+    back,
     s_ref,
     own,
     theirs,
@@ -64,6 +67,8 @@
     recv_sem,
     relay_send_sem,
     relay_recv_sem,
+    back_send_sem,
+    back_recv_sem,
     cut_send_sem,
     cut_recv_sem,
 ):
@@ -81,6 +86,36 @@
     source = lax.rem(me + n_blk - 2 * Z + 1, n_blk)
     landing = lax.rem(me + n_blk - 2 * (Z - 1), n_blk)
     relayer = lax.rem(me + 2 * (Z - 1), n_blk)
+    odd = lax.rem(depth, 2) == 1
+    sends_on = on_chip == 1
+    kind = lax.rem(depth + 1, 2)
+    helps = jnp.logical_and(sends_on, odd)
+
+    def chip(here, by):
+        return lax.rem(here + n_blk + 2 * by, n_blk)
+
+    helper = jnp.where(
+        odd,
+        chip(me, jnp.where(depth == 5, -4, 4)),
+        chip(me, jnp.where(depth <= 2, 5, -3)),
+    )
+    back_sources = (
+        chip(me, jnp.where(depth == 1, 4, -4)),
+        chip(me, jnp.where(depth >= 5, -5, 3)),
+    )
+    back_landings = (
+        chip(me - 1, jnp.where(depth == 1, 5, -3)),
+        chip(me - 1, jnp.where(depth >= 5, -4, 4)),
+    )
+    last_z = lax.rem(depth + Z - 1, Z)
+    back_helper = chip(
+        me + 1,
+        jnp.where(
+            lax.rem(last_z, 2) == 1,
+            jnp.where(last_z == 5, -5, 3),
+            jnp.where(last_z <= 2, 4, -4),
+        ),
+    )
 
     barrier = pltpu.get_barrier_semaphore()
 
@@ -103,6 +138,19 @@
     @pl.when(lands)
     def _():
         greet(relayer)
+
+    @pl.when(sends_on)
+    def _():
+        greet(helper)
+
+    @pl.when(on_chip == 0)
+    def _():
+        greet(back_helper)
+
+    @pl.when(helps)
+    def _():
+        for index in back_sources + back_landings:
+            greet(index)
 
     def columns(q):
         return pl.ds(pl.multiple_of(q * C, C), C)
@@ -162,25 +210,73 @@
             device_id_type=MESH,
         )
 
+    def to_helper(h, k, r):
+        return pltpu.make_async_remote_copy(
+            src_ref=leaving.at[h, h, :, rows(r)],
+            dst_ref=back.at[h, k, RB - 1 - r],
+            send_sem=send_sem.at[h, h, r],
+            recv_sem=back_recv_sem.at[h, k, RB - 1 - r],
+            device_id={"blk": helper},
+            device_id_type=MESH,
+        )
+
+    def from_helper(h, k, r):
+        return pltpu.make_async_remote_copy(
+            src_ref=back.at[h, k, RB - 1 - r],
+            dst_ref=arrived.at[h, h, :, rows(r)],
+            send_sem=back_send_sem.at[h, k, RB - 1 - r],
+            recv_sem=recv_sem.at[h, h, r],
+            device_id={"blk": back_landings[k]},
+            device_id_type=MESH,
+        )
+
+    def help_back(h):
+        @pl.when(helps)
+        def _():
+            for k in (1, 0):
+                for r in range(RB - BACKWARD[h], RB):
+                    to_helper(h, k, r).wait_recv()
+                    from_helper(h, k, r).start()
+
+    def turned(h, q, r):
+        in_first = RB - BACKWARD[h] - TURNED[0] <= r < RB - BACKWARD[h]
+        in_rest = r >= RB - TURNED[1]
+        if in_first and in_rest:
+            return q >= 0
+        return q == h if in_first else q != h if in_rest else q < 0
+
     def send(h, q, r):
         if r < RB - RELAYED:
             onward(h, q, r).start()
-        else:
-
-            @pl.when(turns)
+            return
+        backward = jnp.logical_and(sends_on, q == h) if r >= RB - BACKWARD[h] else q < 0
+        first = jnp.logical_and(turns, turned(h, q, r))
+
+        @pl.when(backward)
+        def _():
+            to_helper(h, kind, r).start()
+
+        @pl.when(first)
+        def _():
+            to_relay(h, q, r).start()
+
+        @pl.when(jnp.logical_not(jnp.logical_or(first, backward)))
+        def _():
+            onward(h, q, r).start()
+
+    def relayed(h, q, act):
+        for r in range(RB - RELAYED, RB):
+
+            @pl.when(jnp.logical_and(relays, turned(h, q, r)))
             def _():
-                to_relay(h, q, r).start()
-
-            @pl.when(jnp.logical_not(turns))
-            def _():
-                onward(h, q, r).start()
+                act(r)
 
     def pass_on(h, q):
-        @pl.when(relays)
-        def _():
-            for r in range(RB - RELAYED, RB):
-                to_relay(h, q, r).wait_recv()
-                from_relay(h, q, r).start()
+        def act(r):
+            to_relay(h, q, r).wait_recv()
+            from_relay(h, q, r).start()
+
+        relayed(h, q, act)
 
     def slopes(q, weight):
         preact = jnp.dot(x_ref[...], weight, preferred_element_type=F32)
@@ -239,10 +335,10 @@
     hop_start(0)
     for r in range(RB):
         xt_ref[rows(r), :] = x_ref[:, rows(r)].T
-    pl.semaphore_wait(
-        barrier,
-        3 + turns.astype(jnp.int32) + 2 * relays.astype(jnp.int32) + lands.astype(jnp.int32),
-    )
+    def one(flag):
+        return flag.astype(jnp.int32)
+
+    pl.semaphore_wait(barrier, 4 + one(turns) + 2 * one(relays) + one(lands) + 4 * one(helps))
     hop_rest(0)
 
     @pl.loop(1, Q)
@@ -252,11 +348,33 @@
 
     cut_grads(0, lambda q: w0_ref.at[q])
 
+    def turn(h, i):
+        return lax.rem(i + h, Q)
+
     for h in range(1, HOPS):
 
+        @pl.loop(0, 2 if h == 1 else Q)
+        def _(i):
+            pass_on(h - 1, turn(h - 1, i))
+
         @pl.loop(0, Q)
-        def _(q):
-            pass_on(h - 1, q)
+        def _(i):
+            q = turn(h, i)
+            if h == 1:
+
+                @pl.when(i == 1)
+                def _():
+                    pass_on(h - 1, turn(h - 1, 2))
+                    pass_on(h - 1, turn(h - 1, 3))
+
+            else:
+
+                @pl.when(i == Q - 1)
+                def _():
+                    @pl.loop(0, Q)
+                    def _(k):
+                        pass_on(h, turn(h, k))
+
             for r in range(RB):
                 onward(h - 1, q, r).wait_recv()
             slopes(q, arrived[h - 1, q, 0])
@@ -270,26 +388,28 @@
                     arrived[h - 1, q, 2, rows(r)].astype(F32),
                 )
 
+        help_back(h - 1)
         cut_grads(h, lambda q: arrived.at[h - 1, q, 0])
         cut_done(h - 1)
 
     def settle(q):
-        pass_on(HOPS - 1, q)
         for r in range(RB):
             onward(HOPS - 1, q, r).wait_recv()
             w_out[rows(r), columns(q)] = arrived[HOPS - 1, q, 0, rows(r)]
             m_out[rows(r), columns(q)] = arrived[HOPS - 1, q, 1, rows(r)].astype(F32)
             v_out[rows(r), columns(q)] = arrived[HOPS - 1, q, 2, rows(r)].astype(F32)
 
+    help_back(HOPS - 1)
+
     @pl.loop(0, 2)
-    def _(q):
-        settle(q)
+    def _(i):
+        settle(turn(HOPS, i))
 
     cut_done(HOPS - 1)
 
     @pl.loop(2, Q)
-    def _(q):
-        settle(q)
+    def _(i):
+        settle(turn(HOPS, i))
 
     for h in range(HOPS):
         cut(h).wait_send()
@@ -299,16 +419,32 @@
             for r in range(RB):
                 onward(h, q, r).wait_send()
 
-            @pl.when(relays)
-            def _():
-                for r in range(RB - RELAYED, RB):
-                    from_relay(h, q, r).wait_send()
+            relayed(h, q, lambda r: from_relay(h, q, r).wait_send())
+
+        @pl.when(helps)
+        def _():
+            for r in range(RB - BACKWARD[h], RB):
+                for k in range(2):
+                    from_helper(h, k, r).wait_send()
+
+
+def deliver(w_in, m_in, v_in, cut_in, w_out, m_out, v_out, cut_out, sem):
+    copies = [
+        pltpu.make_async_copy(m_in, m_out.at[0], sem.at[0]),
+        pltpu.make_async_copy(v_in, v_out.at[0], sem.at[1]),
+        pltpu.make_async_copy(cut_in, cut_out, sem.at[2]),
+        pltpu.make_async_copy(w_in, w_out.at[0], sem.at[3]),
+    ]
+    for copy in copies:
+        copy.start()
+    for copy in copies:
+        copy.wait()
 
 
 def shards(cut_acts, upstream, weights, moment_one, moment_two):
     anywhere = pl.BlockSpec(memory_space=pl.ANY)
     held = pl.BlockSpec(memory_space=pltpu.VMEM)
-    kernel_out, first, second, cuts = pl.pallas_call(
+    trained = pl.pallas_call(
         kernel,
         out_shape=(
             pltpu.VMEM((D, N), BF16),
@@ -328,6 +464,7 @@
             pltpu.VMEM((HOPS, Q, 3, D, C), BF16),
             pltpu.VMEM((HOPS, Q, 3, D, C), BF16),
             pltpu.VMEM((HOPS, Q, RELAYED, 3, RR, C), BF16),
+            pltpu.VMEM((HOPS, 2, 2, 3, RR, C), BF16),
             pltpu.VMEM((Q, ROWS, C), BF16),
             pltpu.VMEM((HOPS, HALF, D), F32),
             pltpu.VMEM((HOPS, HALF, D), BF16),
@@ -341,6 +478,8 @@
             pltpu.SemaphoreType.DMA((HOPS, Q, RB)),
             pltpu.SemaphoreType.DMA((HOPS, Q, RELAYED)),
             pltpu.SemaphoreType.DMA((HOPS, Q, RELAYED)),
+            pltpu.SemaphoreType.DMA((HOPS, 2, 2)),
+            pltpu.SemaphoreType.DMA((HOPS, 2, 2)),
             pltpu.SemaphoreType.DMA((HOPS,)),
             pltpu.SemaphoreType.DMA((HOPS,)),
         ],
@@ -349,7 +488,20 @@
         ),
         name="relay_train",
     )(cut_acts, upstream, weights, moment_one, moment_two)
-    return kernel_out[None], first[None], second[None], cuts
+    return pl.pallas_call(
+        deliver,
+        out_shape=(
+            jax.ShapeDtypeStruct((1, D, N), BF16),
+            jax.ShapeDtypeStruct((1, D, N), F32),
+            jax.ShapeDtypeStruct((1, D, N), F32),
+            jax.ShapeDtypeStruct((HOPS, HALF, D), BF16),
+        ),
+        in_specs=[held] * 4,
+        out_specs=(anywhere,) * 4,
+        scratch_shapes=[pltpu.SemaphoreType.DMA((4,))],
+        compiler_params=pltpu.CompilerParams(vmem_limit_bytes=2**20),
+        name="deliver",
+    )(*trained)
 
 
 def solution(mesh):

time: 119 us -> 109 us (0.916)
  Pallas kernels: 112 us -> 107 us
  local copies, waits for them, and re-layouts: 4.75 us -> 0 us
    pallas_call x1, Pallas kernels: 112 us -> 104 us  [shards(): pl.pallas_call(kernel, out_shape=(pltpu.VMEM((D, N), BF16), pltpu.VMEM((D...]
    unnamed x4 -> x0, local copies, waits for them, and re-layouts: 4.75 us -> none
    pallas_call x0 -> x1, Pallas kernels: none -> 2.86 us  [shards(): pl.pallas_call(deliver, out_shape=(jax.ShapeDtypeStruct((1, D, N), BF16),...]
where the time goes in v2:
time: 109 us; the launch traced here: 107 us
  Pallas kernels  107 us (98%)
    pallas_call x1, Pallas kernels, shards(): pl.pallas_call(kernel, out_shape=(pltpu.VMEM((D, N), BF16), pltpu.VMEM((D...  104 us
    pallas_call x1, Pallas kernels, shards(): pl.pallas_call(deliver, out_shape=(jax.ShapeDtypeStruct((1, D, N), BF16),...  2.86 us

profile of v2, /device:TPU:0, one launch (start us, length us, event | category | flops | bytes accessed | tf_op | source)
XLA Modules:
  0.0 107.2 jit_solution(13101324600835968016)
XLA Ops:
  0.6 103.7 %relay_train.1 = (bf16[1024,512]{1,0:T(8,128)(2,1)S(1)}, f32[1024,512]{1,0:T(8,128)S(1)}, f32[1024,512]{1,0:T(8,128)S(1)}, bf16[3,256,1024]{2,1,0:T(8,128)(2,1)S(1)}) custom-call(bf16[512,1024]{1,0:T(8,128)(2,1)} %acts_hbm.1, bf16[512,512]{1,0:T(8,128)(2,1)} %up_hbm.1, bf16[1,1024,512]{2,1,0:T(8,128)(2,1)} %w_hbm.1, f32[1,1024,512]{2,1,0:T(8,128)} %m_hbm.1, ...), custom_call_target="tpu_custom_call" | custom-call | tf_op jit(solution)/shard_map/relay_train/pallas_call | solution.py:447
  104.3 2.9 %deliver.1 = (bf16[1,1024,512]{2,1,0:T(8,128)(2,1)}, f32[1,1024,512]{2,1,0:T(8,128)}, f32[1,1024,512]{2,1,0:T(8,128)}, bf16[3,256,1024]{2,1,0:T(8,128)(2,1)}) custom-call(bf16[1024,512]{1,0:T(8,128)(2,1)S(1)} %get-tuple-element.8.w_in, f32[1024,512]{1,0:T(8,128)S(1)} %get-tuple-element.9.m_in, f32[1024,512]{1,0:T(8,128)S(1)} %get-tuple-element.10.v_in, ...), custom_call_target="tpu_custom_call" | custom-call | tf_op jit(solution)/shard_map/deliver/pallas_call | solution.py:491

commit v3 on v2

--- a/solution.py
+++ b/solution.py
@@ -19,7 +19,9 @@
 RELAYED = 3
 TURNED = (2, 2)
 Z = 8
-BACKWARD = (2, 2, 1)
+BACKWARD = (2, 2, 0)
+BACKWARD_TURN = (2, 2, 3)
+MOST_BACK = max(BACKWARD_TURN)
 MESH = pl.DeviceIdType.MESH
 F32 = jnp.float32
 BF16 = jnp.bfloat16
@@ -226,20 +228,32 @@
             dst_ref=arrived.at[h, h, :, rows(r)],
             send_sem=back_send_sem.at[h, k, RB - 1 - r],
             recv_sem=recv_sem.at[h, h, r],
-            device_id={"blk": back_landings[k]},
+            device_id={"blk": jnp.where(k == 0, *back_landings)},
             device_id_type=MESH,
         )
 
+    def helped(h, act):
+        early = jnp.where(depth == 5, 0, 1) if h == HOPS - 1 else 1
+        for k in (early, 1 - early):
+            for r in range(RB - BACKWARD_TURN[h], RB):
+                if r >= RB - BACKWARD[h]:
+                    mine = helps
+                else:
+                    mine = jnp.logical_and(helps, jnp.logical_and(depth == 3, k == 0))
+
+                @pl.when(mine)
+                def _():
+                    act(k, r)
+
     def help_back(h):
-        @pl.when(helps)
-        def _():
-            for k in (1, 0):
-                for r in range(RB - BACKWARD[h], RB):
-                    to_helper(h, k, r).wait_recv()
-                    from_helper(h, k, r).start()
+        def act(k, r):
+            to_helper(h, k, r).wait_recv()
+            from_helper(h, k, r).start()
+
+        helped(h, act)
 
     def turned(h, q, r):
-        in_first = RB - BACKWARD[h] - TURNED[0] <= r < RB - BACKWARD[h]
+        in_first = RB - BACKWARD[h] - TURNED[0] <= r < RB - BACKWARD_TURN[h]
         in_rest = r >= RB - TURNED[1]
         if in_first and in_rest:
             return q >= 0
@@ -249,7 +263,12 @@
         if r < RB - RELAYED:
             onward(h, q, r).start()
             return
-        backward = jnp.logical_and(sends_on, q == h) if r >= RB - BACKWARD[h] else q < 0
+        if r >= RB - BACKWARD[h]:
+            backward = jnp.logical_and(sends_on, q == h)
+        elif r >= RB - BACKWARD_TURN[h]:
+            backward = jnp.logical_and(turns, q == h)
+        else:
+            backward = q < 0
         first = jnp.logical_and(turns, turned(h, q, r))
 
         @pl.when(backward)
@@ -421,11 +440,7 @@
 
             relayed(h, q, lambda r: from_relay(h, q, r).wait_send())
 
-        @pl.when(helps)
-        def _():
-            for r in range(RB - BACKWARD[h], RB):
-                for k in range(2):
-                    from_helper(h, k, r).wait_send()
+        helped(h, lambda k, r: from_helper(h, k, r).wait_send())
 
 
 def deliver(w_in, m_in, v_in, cut_in, w_out, m_out, v_out, cut_out, sem):
@@ -464,7 +479,7 @@
             pltpu.VMEM((HOPS, Q, 3, D, C), BF16),
             pltpu.VMEM((HOPS, Q, 3, D, C), BF16),
             pltpu.VMEM((HOPS, Q, RELAYED, 3, RR, C), BF16),
-            pltpu.VMEM((HOPS, 2, 2, 3, RR, C), BF16),
+            pltpu.VMEM((HOPS, 2, MOST_BACK, 3, RR, C), BF16),
             pltpu.VMEM((Q, ROWS, C), BF16),
             pltpu.VMEM((HOPS, HALF, D), F32),
             pltpu.VMEM((HOPS, HALF, D), BF16),
@@ -478,8 +493,8 @@
             pltpu.SemaphoreType.DMA((HOPS, Q, RB)),
             pltpu.SemaphoreType.DMA((HOPS, Q, RELAYED)),
             pltpu.SemaphoreType.DMA((HOPS, Q, RELAYED)),
-            pltpu.SemaphoreType.DMA((HOPS, 2, 2)),
-            pltpu.SemaphoreType.DMA((HOPS, 2, 2)),
+            pltpu.SemaphoreType.DMA((HOPS, 2, MOST_BACK)),
+            pltpu.SemaphoreType.DMA((HOPS, 2, MOST_BACK)),
             pltpu.SemaphoreType.DMA((HOPS,)),
             pltpu.SemaphoreType.DMA((HOPS,)),
         ],

time: 109 us -> 108 us (level); the launches traced: 107 us -> 108 us
  no operation moved by 1% of the time
where the time goes in v3:
time: 108 us
  Pallas kernels  107 us (99%)
    pallas_call x1, Pallas kernels, shards(): pl.pallas_call(kernel, out_shape=(pltpu.VMEM((D, N), BF16), pltpu.VMEM((D...  104 us
    pallas_call x1, Pallas kernels, shards(): pl.pallas_call(deliver, out_shape=(jax.ShapeDtypeStruct((1, D, N), BF16),...  2.86 us

profile of v3, /device:TPU:0, one launch (start us, length us, event | category | flops | bytes accessed | tf_op | source)
XLA Modules:
  0.0 107.6 jit_solution(3862397914363718900)
XLA Ops:
  0.6 104.1 %relay_train.1 = (bf16[1024,512]{1,0:T(8,128)(2,1)S(1)}, f32[1024,512]{1,0:T(8,128)S(1)}, f32[1024,512]{1,0:T(8,128)S(1)}, bf16[3,256,1024]{2,1,0:T(8,128)(2,1)S(1)}) custom-call(bf16[512,1024]{1,0:T(8,128)(2,1)} %acts_hbm.1, bf16[512,512]{1,0:T(8,128)(2,1)} %up_hbm.1, bf16[1,1024,512]{2,1,0:T(8,128)(2,1)} %w_hbm.1, f32[1,1024,512]{2,1,0:T(8,128)} %m_hbm.1, ...), custom_call_target="tpu_custom_call" | custom-call | tf_op jit(solution)/shard_map/relay_train/pallas_call | solution.py:462
  104.7 2.9 %deliver.1 = (bf16[1,1024,512]{2,1,0:T(8,128)(2,1)}, f32[1,1024,512]{2,1,0:T(8,128)}, f32[1,1024,512]{2,1,0:T(8,128)}, bf16[3,256,1024]{2,1,0:T(8,128)(2,1)}) custom-call(bf16[1024,512]{1,0:T(8,128)(2,1)S(1)} %get-tuple-element.8.w_in, f32[1024,512]{1,0:T(8,128)S(1)} %get-tuple-element.9.m_in, f32[1024,512]{1,0:T(8,128)S(1)} %get-tuple-element.10.v_in, ...), custom_call_target="tpu_custom_call" | custom-call | tf_op jit(solution)/shard_map/deliver/pallas_call | solution.py:506

commit v4 on v3

--- a/solution.py
+++ b/solution.py
@@ -428,7 +428,7 @@
 
     @pl.loop(2, Q)
     def _(i):
-        settle(turn(HOPS, i))
+        settle(Q - i)
 
     for h in range(HOPS):
         cut(h).wait_send()

time: 108 us -> 108 us (level)
  no operation moved by 1% of the time
where the time goes in v4:
time: 108 us
  Pallas kernels  107 us (99%)
    pallas_call x1, Pallas kernels, shards(): pl.pallas_call(kernel, out_shape=(pltpu.VMEM((D, N), BF16), pltpu.VMEM((D...  104 us
    pallas_call x1, Pallas kernels, shards(): pl.pallas_call(deliver, out_shape=(jax.ShapeDtypeStruct((1, D, N), BF16),...  2.86 us

profile of v4, /device:TPU:0, one launch (start us, length us, event | category | flops | bytes accessed | tf_op | source)
XLA Modules:
  0.0 107.6 jit_solution(8857512015722739471)
XLA Ops:
  0.6 104.1 %relay_train.1 = (bf16[1024,512]{1,0:T(8,128)(2,1)S(1)}, f32[1024,512]{1,0:T(8,128)S(1)}, f32[1024,512]{1,0:T(8,128)S(1)}, bf16[3,256,1024]{2,1,0:T(8,128)(2,1)S(1)}) custom-call(bf16[512,1024]{1,0:T(8,128)(2,1)} %acts_hbm.1, bf16[512,512]{1,0:T(8,128)(2,1)} %up_hbm.1, bf16[1,1024,512]{2,1,0:T(8,128)(2,1)} %w_hbm.1, f32[1,1024,512]{2,1,0:T(8,128)} %m_hbm.1, ...), custom_call_target="tpu_custom_call" | custom-call | tf_op jit(solution)/shard_map/relay_train/pallas_call | solution.py:462
  104.8 2.9 %deliver.1 = (bf16[1,1024,512]{2,1,0:T(8,128)(2,1)}, f32[1,1024,512]{2,1,0:T(8,128)}, f32[1,1024,512]{2,1,0:T(8,128)}, bf16[3,256,1024]{2,1,0:T(8,128)(2,1)}) custom-call(bf16[1024,512]{1,0:T(8,128)(2,1)S(1)} %get-tuple-element.8.w_in, f32[1024,512]{1,0:T(8,128)S(1)} %get-tuple-element.9.m_in, f32[1024,512]{1,0:T(8,128)S(1)} %get-tuple-element.10.v_in, ...), custom_call_target="tpu_custom_call" | custom-call | tf_op jit(solution)/shard_map/deliver/pallas_call | solution.py:506
